TPU v7x, 16 devices: a whole 2x2x2 slice. The times are simulated.
16 devices in a mesh: dp: 4 (over z, y), ep: 4 (over x, core).
Axes of the slice: x: 2, y: 2, z: 2, core: 2. Of those that a mesh axis runs over, the one named last changes fastest.
Arguments:
- x_tok: bfloat16 [1024, 1536], P(('dp', 'ep')), parts along dimension 0
- topk_idx: int32 [1024, 6], P(('dp', 'ep')), parts along dimension 0
- topk_w: float32 [1024, 6], P(('dp', 'ep')), parts along dimension 0
- w_in: bfloat16 [64, 1536, 512], P('ep')
- w_out: bfloat16 [64, 512, 1536], P('ep')
- shared_in: bfloat16 [1536, 1024], replicated
- shared_out: bfloat16 [1024, 1536], replicated
Outputs:
- output: bfloat16 [1024, 1536], P(('dp', 'ep')), parts along dimension 0
There are 4 independent parts. A program takes and returns all parts, laid end to end along the dimension named above; an argument that names none is the same for every part.
All inputs are finite; a program needn't handle non-finite values.
Results may differ from a plain program's by a relative error of at most 0.001.
Values are sent between devices in bfloat16 or wider.
A program may use at most 1 GiB of HBM per device.

v0:
```python
import functools
import math

import jax
import jax.numpy as jnp
from jax import lax
from jax.experimental import pallas as pl
from jax.experimental.pallas import tpu as pltpu
from jax.sharding import PartitionSpec as P

MESH = pl.DeviceIdType.MESH
LOAD_MULT = 3
SPOTS = (0, 2, 4, 6, 8, 10, 12, 13)
DIRECT = 128
EARLY = 12
LAG = 2
VMEM_LIMIT = 62500000
scope = jax.named_scope
COLS = 256
GELU_A = math.sqrt(2.0 / math.pi)
GELU_B = GELU_A * 0.044715


def gelu(z):
    return 0.5 * z * (1.0 + jnp.tanh(z * (GELU_A + GELU_B * (z * z))))


def dot(a, b):
    return jnp.dot(a, b, preferred_element_type=jnp.float32)


def layer_kernel(
    dims,
    x_hbm, idx_hbm, gate_hbm, win_hbm, wout_hbm, sin_hbm, sout_hbm,
    y_ref,
    x_all, win, wout, idx_all, gate_all, disp, comb, rows_in, acc, hidden, rows_out,
    part, sib_part, sib_fwd, link_out, link_in, direct_a, direct_b, shared_h, shared_u,
    *sems):
    (fence_sem, small_sem, x_sem, win_sem, wout_sem, shared_sem,
     meta_send, meta_recv, xl_send, xl_recv, xs_send, xs_recv, xf_send, xf_recv,
     ps_send, ps_recv, pf_send, pf_recv, pl_send, pl_recv, direct_send, direct_recv) = sems
    tok, top_k, local_e, slot, tokens = dims
    d_model, ff = win_hbm.shape[1], win_hbm.shape[2]
    chunks = d_model // COLS
    me = lax.axis_index('ep')
    chip, core = lax.div(me, 2), lax.rem(me, 2)
    sib = chip * 2 + (1 - core)
    partner = (1 - chip) * 2 + (1 - core)
    other = (1 - chip) * 2 + core
    peers = (sib, partner, other)

    def rows_of(dev):
        return pl.ds(pl.multiple_of(dev * tok, tok), tok)

    def remote(src, dst, send, recv, dev):
        return pltpu.make_async_remote_copy(
            src_ref=src, dst_ref=dst, send_sem=send, recv_sem=recv,
            device_id={'ep': dev}, device_id_type=MESH)

    def fence():
        pl.semaphore_signal(fence_sem, 1)
        pl.semaphore_wait(fence_sem, 1)

    idx_cp = pltpu.make_async_copy(idx_hbm, idx_all.at[me], small_sem.at[0])
    gate_cp = pltpu.make_async_copy(gate_hbm, gate_all.at[me], small_sem.at[1])
    x_cps = [pltpu.make_async_copy(x_hbm.at[:, pl.ds(k * COLS, COLS)], x_all.at[k, rows_of(me)], x_sem.at[k]) for k in range(chunks)]
    win_cps = [pltpu.make_async_copy(win_hbm.at[:, pl.ds(k * COLS, COLS), :], win.at[k], win_sem.at[k]) for k in range(chunks)]
    wout_cps = [pltpu.make_async_copy(wout_hbm.at[:, :, pl.ds(n * COLS, COLS)], wout.at[n], wout_sem.at[n]) for n in range(chunks)]
    barrier = pltpu.get_barrier_semaphore()
    for peer in peers:
        pl.semaphore_signal(barrier, inc=1, device_id={'ep': peer}, device_id_type=MESH)
    for cp in [idx_cp, gate_cp] + x_cps:
        cp.start()
    for cp in win_cps + wout_cps:
        fence()
        cp.start()

    with scope('w_small'):
        for cp in [idx_cp, gate_cp] + x_cps:
            cp.wait()
    with scope('w_barrier'):
        pl.semaphore_wait(barrier, 3)
    meta_cps = []
    for r, peer in enumerate(peers):
        meta_cps.append(remote(idx_all.at[me], idx_all.at[me], meta_send.at[r], meta_recv.at[r], peer))
        meta_cps.append(remote(gate_all.at[me], gate_all.at[me], meta_send.at[3 + r], meta_recv.at[3 + r], peer))
    for cp in meta_cps:
        cp.start()
    xl_cps, xs_cps, xf_cps = [], [], []
    for k in range(chunks):
        mine, theirs = x_all.at[k, rows_of(me)], x_all.at[k, rows_of(partner)]
        xl_cps.append(remote(mine, mine, xl_send.at[k], xl_recv.at[k], partner))
        xs_cps.append(remote(mine, mine, xs_send.at[k], xs_recv.at[k], sib))
        xf_cps.append(remote(theirs, theirs, xf_send.at[k], xf_recv.at[k], sib))
    for k in range(chunks):
        xl_cps[k].start()
        xs_cps[k].start()

    with scope('w_meta'):
        for cp in meta_cps:
            cp.wait_recv()
    group = tokens // tok
    idx_t = jnp.concatenate([idx_all[s] for s in range(group)], axis=1)
    gate_t = jnp.concatenate([gate_all[s] for s in range(group)], axis=1).astype(jnp.bfloat16).astype(jnp.float32)
    expert_id = lax.broadcasted_iota(jnp.int32, (local_e, tokens), 0) + me * local_e
    picked = jnp.zeros((local_e, tokens), jnp.float32)
    gates = jnp.zeros((local_e, tokens), jnp.float32)
    for j in range(top_k):
        hit = idx_t[j:j + 1, :] == expert_id
        picked = picked + jnp.where(hit, 1.0, 0.0)
        gates = gates + jnp.where(hit, gate_t[j:j + 1, :], 0.0)
    before = (lax.broadcasted_iota(jnp.int32, (tokens, tokens), 0) < lax.broadcasted_iota(jnp.int32, (tokens, tokens), 1))
    rank = dot(picked.astype(jnp.bfloat16), jnp.where(before, 1.0, 0.0).astype(jnp.bfloat16))
    rank = jnp.where(picked > 0.5, rank, -1.0)
    slot_id = lax.broadcasted_iota(jnp.int32, (slot, tokens), 0).astype(jnp.float32)
    for e in range(local_e):
        here = slot_id == rank[e:e + 1, :]
        disp[pl.ds(e * slot, slot), :] = jnp.where(here, 1.0, 0.0).astype(jnp.bfloat16)
        rows_out[pl.ds(e * slot, slot), :] = jnp.where(here, gates[e:e + 1, :], 0.0).astype(jnp.bfloat16)
    for i in range(local_e * slot // 256):
        comb[:, pl.ds(i * 256, 256)] = rows_out[pl.ds(i * 256, 256), :].T

    def forward(k):
        with scope(f'w_xl{k}'):
            xl_cps[k].wait_recv()
        xf_cps[k].start()

    def await_rows(k):
        with scope(f'w_xs{k}'):
            xs_cps[k].wait_recv()
        with scope(f'w_xf{k}'):
            xf_cps[k].wait_recv()

    def gather(k, piece, pieces):
        m = local_e * slot // pieces
        r = pl.ds(piece * m, m)
        rows_in[k % 3, r, :] = dot(disp[r, :], x_all[k]).astype(jnp.bfloat16)

    forward(0)
    forward(1)
    await_rows(0)
    gather(0, 0, 2)
    gather(0, 1, 2)
    def first(k, e):
        r = pl.ds(e * slot, slot)
        term = dot(rows_in[k % 3, r, :], win[k, e])
        if k == 0:
            acc[r, :] = term
        elif k + 2 < chunks:
            acc[r, :] = acc[r, :] + term
        else:
            term = term + dot(rows_in[(k + 1) % 3, r, :], win[k + 1, e])
            hidden[r, :] = gelu(acc[r, :] + term).astype(jnp.bfloat16)

    def second(n, e, total):
        r = pl.ds(e * slot, slot)
        rows_out[r, :] = dot(hidden[r, :], wout[n, e]).astype(jnp.bfloat16)
        ready = e * slot // COLS if e + 1 < local_e else local_e * slot // COLS
        for i in range(max(e - 1, 0) * slot // COLS, ready):
            c = pl.ds(i * COLS, COLS)
            term = dot(comb[:, c], rows_out[c, :])
            total = term if total is None else total + term
        return total

    for k in range(chunks - 2):
        if k + 3 < chunks:
            forward(k + 2)
        await_rows(k + 1)
        if k + 4 == chunks:
            forward(chunks - 1)
        if k + 3 == chunks:
            await_rows(chunks - 1)
        with scope(f'w_win{k}'):
            win_cps[k].wait()
        for e in range(local_e):
            first(k, e)
            if e in SPOTS:
                gather(k + 1, SPOTS.index(e), len(SPOTS))
                if k + 3 == chunks:
                    gather(chunks - 1, SPOTS.index(e), len(SPOTS))
    for k in range(chunks - 2, chunks):
        with scope(f'w_win{k}'):
            win_cps[k].wait()
    with scope('w_wout0'):
        wout_cps[0].wait()
    total = None
    for e in range(local_e + LAG):
        if e < local_e:
            first(chunks - 2, e)
        if e >= LAG:
            total = second(0, e - LAG, total)

    shared_cps = []

    def load_shared():
        for j in range(2):
            shared_cps.append(pltpu.make_async_copy(sin_hbm.at[:, :, pl.ds(j * ff, ff)], win.at[:, j], shared_sem.at[j]))
        for j in range(3):
            shared_cps.append(pltpu.make_async_copy(
                sout_hbm.at[:, :, pl.ds(j * ff, ff)], win.at[pl.ds(0, sout_hbm.shape[0]), 2 + j], shared_sem.at[2 + j]))
        for cp in shared_cps:
            cp.start()

    head, rest = pl.ds(0, DIRECT), pl.ds(DIRECT, COLS - DIRECT)
    da_cp = remote(part.at[0, rows_of(partner), head], direct_a, direct_send.at[0], direct_recv.at[0], partner)
    db_cp = remote(part.at[0, rows_of(other), head], direct_b, direct_send.at[1], direct_recv.at[1], other)
    ps_cps = [remote(part.at[n, rows_of(sib)], sib_part.at[n], ps_send.at[n], ps_recv.at[n], sib) for n in range(chunks)]
    pf_cps = [remote(part.at[0, rows_of(other), rest], sib_fwd.at[0, :, rest], pf_send.at[0], pf_recv.at[0], sib)]
    pl_cps = [remote(link_out.at[0, :, rest], link_in.at[0, :, rest], pl_send.at[0], pl_recv.at[0], partner)]
    for n in range(1, chunks):
        pf_cps.append(remote(part.at[n, rows_of(other)], sib_fwd.at[n], pf_send.at[n], pf_recv.at[n], sib))
        pl_cps.append(remote(link_out.at[n], link_in.at[n], pl_send.at[n], pl_recv.at[n], partner))

    def send_back(n):
        with scope(f'w_pf{n}'):
            pf_cps[n].wait_recv()
        c = pl.ds(0, COLS) if n else rest
        link_out[n, :, c] = part[n, rows_of(partner), c] + sib_fwd[n, :, c]
        pl_cps[n].start()

    for n in range(chunks):
        if n:
            with scope(f'w_wout{n}'):
                wout_cps[n].wait()
        if n:
            total = None
            for e in range(local_e):
                if n == 1 and e == EARLY:
                    send_back(0)
                total = second(n, e, total)
        part[n] = total
        pf_cps[n].start()
        if n == 0:
            da_cp.start()
            db_cp.start()
        ps_cps[n].start()
        if n == 0:
            load_shared()
        if n > 1:
            send_back(n - 1)
    send_back(chunks - 1)

    with scope('w_shared'):
        for cp in shared_cps:
            cp.wait()
    for j in range(2):
        s = dot(x_all[0, rows_of(me), :], win[0, j])
        for k in range(1, chunks):
            s = s + dot(x_all[k, rows_of(me), :], win[k, j])
        shared_h[:, pl.ds(j * ff, ff)] = gelu(s).astype(jnp.bfloat16)
    for j in range(3):
        u = dot(shared_h[:, 0:COLS], win[0, 2 + j])
        for i in range(1, 4):
            u = u + dot(shared_h[:, pl.ds(i * COLS, COLS)], win[i, 2 + j])
        shared_u[:, pl.ds(j * ff, ff)] = u

    for n in range(chunks):
        with scope(f'w_ps{n}'):
            ps_cps[n].wait_recv()
        mine = shared_u[:, pl.ds(n * COLS, COLS)] + part[n, rows_of(me), :] + sib_part[n]
        with scope(f'w_pl{n}'):
            pl_cps[n].wait_recv()
        if n:
            y_ref[:, pl.ds(n * COLS, COLS)] = (mine + link_in[n]).astype(jnp.bfloat16)
        else:
            da_cp.wait_recv()
            db_cp.wait_recv()
            y_ref[:, head] = (mine[:, :DIRECT] + (direct_a[...] + direct_b[...])).astype(jnp.bfloat16)
            y_ref[:, rest] = (mine[:, DIRECT:] + link_in[0, :, rest]).astype(jnp.bfloat16)
    with scope('w_sends'):
        for cp in [da_cp, db_cp] + meta_cps + xl_cps + xs_cps + xf_cps + ps_cps + pf_cps + pl_cps:
            cp.wait_send()


def solution(mesh):
    group = mesh.shape['ep']

    def local_layer(x_loc, idx_loc, gate_loc, w_in, w_out, shared_in, shared_out):
        tok, top_k = idx_loc.shape
        local_e, d_model, ff = w_in.shape
        fs = shared_in.shape[1]
        tokens = tok * group
        cap = min(tok, LOAD_MULT * tok * top_k // (local_e * group))
        slot = -(-cap * group // 16) * 16
        total = local_e * slot
        chunks = d_model // COLS
        bf16, f32 = jnp.bfloat16, jnp.float32
        dma = pltpu.SemaphoreType.DMA
        scratch = [
            pltpu.VMEM((chunks, tokens, COLS), bf16),
            pltpu.VMEM((chunks, local_e, COLS, ff), bf16),
            pltpu.VMEM((chunks, local_e, ff, COLS), bf16),
            pltpu.VMEM((group, top_k, tok), jnp.int32),
            pltpu.VMEM((group, top_k, tok), f32),
            pltpu.VMEM((total, tokens), bf16),
            pltpu.VMEM((tokens, total), bf16),
            pltpu.VMEM((3, total, COLS), bf16),
            pltpu.VMEM((total, ff), f32),
            pltpu.VMEM((total, ff), bf16),
            pltpu.VMEM((total, COLS), bf16),
            pltpu.VMEM((chunks, tokens, COLS), f32),
            pltpu.VMEM((chunks, tok, COLS), f32),
            pltpu.VMEM((chunks, tok, COLS), f32),
            pltpu.VMEM((chunks, tok, COLS), f32),
            pltpu.VMEM((chunks, tok, COLS), f32),
            pltpu.VMEM((tok, DIRECT), f32),
            pltpu.VMEM((tok, DIRECT), f32),
            pltpu.VMEM((tok, fs), bf16),
            pltpu.VMEM((tok, d_model), f32),
        ]
        sems = [pltpu.SemaphoreType.REGULAR, dma((2,)), dma((chunks,)), dma((chunks,)), dma((chunks,)), dma((5,)), dma((6,)), dma((6,))]
        sems += [dma((chunks,))] * 12 + [dma((2,))] * 2

        def kernel(*refs):
            pl.run_scoped(functools.partial(layer_kernel, (tok, top_k, local_e, slot, tokens), *refs), *sems)

        any_spec = pl.BlockSpec(memory_space=pltpu.HBM)
        return pl.pallas_call(
            kernel,
            out_shape=pltpu.VMEM((tok, d_model), bf16),
            in_specs=[any_spec] * 7,
            out_specs=pl.BlockSpec(memory_space=pltpu.VMEM),
            scratch_shapes=scratch,
            compiler_params=pltpu.CompilerParams(
                collective_id=0, has_side_effects=True, vmem_limit_bytes=VMEM_LIMIT),
        )(x_loc, idx_loc.T, gate_loc.T, w_in, w_out,
          shared_in.reshape(chunks, COLS, fs), shared_out.reshape(fs // COLS, COLS, d_model))

    tok_spec = P(('dp', 'ep'), None)
    expert_spec = P('ep', None, None)
    whole_spec = P(None, None)
    return jax.shard_map(
        local_layer, mesh=mesh,
        in_specs=(tok_spec, tok_spec, tok_spec, expert_spec, expert_spec, whole_spec, whole_spec),
        out_specs=tok_spec, check_vma=False)
```

profile of v0, /device:TPU:0, one launch (start us, length us, event | category | flops | bytes accessed | tf_op | source)
XLA Modules:
  0.0 26.9 jit_solution(16534195355771304319)
XLA Ops:
  0.0 26.2 %shard_map.73 = bf16[64,1536]{1,0:T(8,128)(2,1)S(1)} custom-call(bf16[64,1536]{1,0:T(8,128)(2,1)} %refs_0_.1, s32[6,64]{1,0:T(8,128)} %bitcast.6, f32[6,64]{1,0:T(8,128)} %bitcast.7, bf16[16,1536,512]{2,1,0:T(8,128)(2,1)} %refs_3_.1, bf16[16,512,1536]{2,1,0:T(8,128)(2,1)} %refs_4_.1, bf16[6,256,1024]{2,1,0:T(8,128)(2,1)} %bitcast.4, ...), custom_call_target="tpu_custom_call" | custom-call | tf_op jit(solution)/shard_map/pallas_call | solution.py:318
  26.2 0.7 %copy.9 = bf16[64,1536]{1,0:T(8,128)(2,1)} copy(bf16[64,1536]{1,0:T(8,128)(2,1)S(1)} %shard_map.73) | data formatting | bytes 393216
where the time goes:
time: 27 us; the launch traced here: 26.9 us
  Pallas kernels  26.2 us (97%)
  local copies, waits for them, and re-layouts  0.68 us (3%)
    pallas_call x1, Pallas kernels, local_layer(): pl.pallas_call(kernel, out_shape=pltpu.VMEM((tok, d_model), bf16), in_spe...  26.2 us
    unnamed x1, local copies, waits for them, and re-layouts  0.68 us

commit v1 on v0

--- a/solution.py
+++ b/solution.py
@@ -13,7 +13,7 @@
 SPOTS = (0, 2, 4, 6, 8, 10, 12, 13)
 DIRECT = 128
 EARLY = 12
-LAG = 2
+LAG = 4
 VMEM_LIMIT = 62500000
 scope = jax.named_scope
 COLS = 256
@@ -225,8 +225,8 @@
         if n:
             total = None
             for e in range(local_e):
-                if n == 1 and e == EARLY:
-                    send_back(0)
+                if n == 2 and e == EARLY:
+                    send_back(1)
                 total = second(n, e, total)
         part[n] = total
         pf_cps[n].start()
@@ -236,7 +236,7 @@
         ps_cps[n].start()
         if n == 0:
             load_shared()
-        if n > 1:
+        if n and n != 2:
             send_back(n - 1)
     send_back(chunks - 1)
 

time: 27 us -> 27 us (level)
  no operation moved by 1% of the time
where the time goes in v1:
time: 27 us; the launch traced here: 26.9 us
  Pallas kernels  26.2 us (97%)
  local copies, waits for them, and re-layouts  0.68 us (3%)
    pallas_call x1, Pallas kernels, local_layer(): pl.pallas_call(kernel, out_shape=pltpu.VMEM((tok, d_model), bf16), in_spe...  26.2 us
    unnamed x1, local copies, waits for them, and re-layouts  0.68 us

profile of v1, /device:TPU:0, one launch (start us, length us, event | category | flops | bytes accessed | tf_op | source)
XLA Modules:
  0.0 26.9 jit_solution(15839713291839927065)
XLA Ops:
  0.0 26.2 %shard_map.73 = bf16[64,1536]{1,0:T(8,128)(2,1)S(1)} custom-call(bf16[64,1536]{1,0:T(8,128)(2,1)} %refs_0_.1, s32[6,64]{1,0:T(8,128)} %bitcast.6, f32[6,64]{1,0:T(8,128)} %bitcast.7, bf16[16,1536,512]{2,1,0:T(8,128)(2,1)} %refs_3_.1, bf16[16,512,1536]{2,1,0:T(8,128)(2,1)} %refs_4_.1, bf16[6,256,1024]{2,1,0:T(8,128)(2,1)} %bitcast.4, ...), custom_call_target="tpu_custom_call" | custom-call | tf_op jit(solution)/shard_map/pallas_call | solution.py:318
  26.2 0.7 %copy.9 = bf16[64,1536]{1,0:T(8,128)(2,1)} copy(bf16[64,1536]{1,0:T(8,128)(2,1)S(1)} %shard_map.73) | data formatting | bytes 393216
